TPU v7x, 32 devices: a whole 2x2x4 slice. The times are simulated.
32 devices in a mesh: gx: 4 (over y, x), gy: 8 (over z, core).
Axes of the slice: x: 2, y: 2, z: 4, core: 2. Of those that a mesh axis runs over, the one named last changes fastest.
Arguments:
- tile_flux: bfloat16 [4, 12, 8, 131072], P(None, None, None, ('gx', 'gy')), may hold values from -6 to 6
- tile_frac: float32 [8, 131072], P(None, ('gx', 'gy')), may hold values from 0.02 to 1
- weights: bfloat16 [32, 7, 16, 256, 128], P(('gx', 'gy')), may hold values from -0.049804688 to 0.14941406
- block_row: int32 [32, 7, 16], P(('gx', 'gy')), may hold values from 0 to 47
- block_col: int32 [32, 7, 16], P(('gx', 'gy')), may hold values from 0 to 31
- send_counts: int32 [32, 7], P(('gx', 'gy')), may hold values from 1 to 16, as said below
Outputs:
- atm_flux: float32 [4, 12, 393216], P(None, None, ('gx', 'gy'))
Inputs may be any that keep to these rules, and one draw needn't show every extreme that they name: `send_counts`: live slots of a device at an offset; some device has all 7 offsets at 16, and some device receives 16 live slots from every offset.
All inputs are finite; a program needn't handle non-finite values.
Results may differ from a plain program's by a relative error of at most 0.0029.
Values sent between devices are 32-bit elements; how exact they have to be, the bound alone decides.
A program may use at most 128 MiB of HBM per device.

v0:
```python
import jax
import jax.numpy as jnp
from jax import lax
from jax.sharding import PartitionSpec as P

AB_DEV = 48


def shifted(value, axis, steps):
    count = lax.axis_size(axis)
    pairs = [(source, (source + steps) % count) for source in range(count)]
    return lax.ppermute(value, axis, pairs)


def settle(partial_value, targets, blocks_here):
    onehot = (targets[:, None] == jnp.arange(blocks_here, dtype=jnp.float32)[None, :]).astype(
        jnp.float32
    )
    return jnp.einsum("kj,kfr->jfr", onehot, partial_value, precision=lax.Precision.HIGHEST)


def on_device(tile_flux, tile_frac, weights, block_row, block_col, send_counts):
    num_steps = tile_flux.shape[0]
    num_kinds = tile_flux.shape[1]
    num_flux = num_steps * num_kinds
    num_off = weights.shape[1]
    slots = weights.shape[2]
    block_rows = weights.shape[3]
    block_cols = weights.shape[4]
    reach_side = num_off // 2
    frac_sum = jnp.sum(tile_frac, axis=0)
    merged = (
        jnp.sum(tile_flux.astype(jnp.float32) * tile_frac[None, None], axis=2) / frac_sum
    ).astype(jnp.bfloat16)
    land_blocks = merged.reshape(num_flux, -1, block_cols)
    picked = jnp.take(land_blocks, block_col[0].reshape(-1), axis=1)
    picked = picked.reshape(num_flux, num_off, slots, block_cols)
    partial_value = jnp.einsum(
        "okrc,fokc->okfr", weights[0], picked, preferred_element_type=jnp.float32
    )
    active = (jnp.arange(slots, dtype=jnp.int32)[None, :] < send_counts[0][:, None]).astype(
        jnp.float32
    )
    partial_value = partial_value * active[:, :, None, None]
    targets = block_row[0].astype(jnp.float32)
    totals = settle(partial_value[reach_side], targets[reach_side], AB_DEV)
    for offset in range(num_off):
        if offset != reach_side:
            arrived, arrived_rows = shifted(
                (partial_value[offset], targets[offset]), ("gx", "gy"), offset - reach_side
            )
            totals = totals + settle(arrived, arrived_rows, AB_DEV)
    return totals.transpose(1, 0, 2).reshape(num_steps, num_kinds, AB_DEV * block_rows)


def solution(mesh):
    return jax.shard_map(
        on_device,
        mesh=mesh,
        in_specs=(
            P(None, None, None, ("gx", "gy")),
            P(None, ("gx", "gy")),
            P(("gx", "gy"), None, None, None, None),
            P(("gx", "gy"), None, None),
            P(("gx", "gy"), None, None),
            P(("gx", "gy"), None),
        ),
        out_specs=P(None, None, ("gx", "gy")),
        check_vma=False,
    )
```

profile of v0, /device:TPU:0, one launch (start us, length us, event | category | flops | bytes accessed | tf_op | source)
XLA Modules:
  0.0 137.1 jit_solution(5694432180098506802)
XLA Ops:
  0.0 0.7 reduce
  0.7 0.1 reshape_squeeze.6
  0.8 0.8 fusion.45
  1.6 0.9 reduce_sum.22
  2.5 4.0 %multiply_reduce_fusion = f32[4,12,4096]{2,1,0:T(8,128)S(1)} fusion(bf16[4,12,8,4096]{3,2,1,0:T(8,128)(2,1)} %param.6, f32[8,4096]{1,0:T(8,128)} %param.7), kind=kLoop, calls=%fused_computation.3 | loop fusion | flops 4521984 | bytes 4063232 | tf_op jit(solution)/shard_map/reduce_sum | solution.py:33
  6.5 0.2 reduce_sum.21
  6.7 0.5 fusion.22
  7.2 0.8 gather_fusion
  8.0 5.8 %broadcast_multiply_fusion = f32[7,16,48,256]{3,2,1,0:T(8,128)S(1)} fusion(f32[7,16]{1,0:T(8,128)S(1)} %get-tuple-element.19, bf16[1,7,16,256,128]{4,3,2,1,0:T(8,128)(2,1)} %param.8, bf16[48,7,16,128]{3,0,2,1:T(8,128)(2,1)S(1)} %bitcast.67, pred[7,16]{1,0:T(8,128)(4,1)S(1)} %get-tuple-element.20), kind=kOutput, calls=%fused_computation.4 | convolution fusion | flops 354385920 | bytes 14221872 | tf_op jit(solution)/shard_map/okrc,fokc->okfr/dot_general | solution.py:38
  13.8 0.4 slice_bitcast_fusion
  14.2 5.4 %collective-permute-start.1 = (f32[16,48,256]{2,1,0:T(8,128)S(1)}, f32[16,48,256]{2,1,0:T(8,128)S(1)}, u32[]{:S(2)}, u32[]{:S(2)}) collective-permute-start(f32[16,48,256]{2,1,0:T(8,128)S(1)} %get-tuple-element.10), channel_id=1, source_target_pairs={{0,29},{1,30},{2,31},{3,0},{4,1},{5,2},{6,3},{7,4},{8,5},{9,6},{10... | collective-permute-start | bytes 2359304 | tf_op jit(solution)/shard_map/ppermute | solution.py:12
  19.7 1.6 %collective-permute-start.3 = (f32[16,48,256]{2,1,0:T(8,128)S(1)}, f32[16,48,256]{2,1,0:T(8,128)S(1)}, u32[]{:S(2)}, u32[]{:S(2)}) collective-permute-start(f32[16,48,256]{2,1,0:T(8,128)S(1)} %get-tuple-element.9), channel_id=1, source_target_pairs={{0,30},{1,31},{2,0},{3,1},{4,2},{5,3},{6,4},{7,5},{8,6},{9,7},{10,... | collective-permute-start | bytes 2359304 | tf_op jit(solution)/shard_map/ppermute | solution.py:12
  21.3 1.5 %collective-permute-start.10 = (f32[16]{0:T(128)S(1)}, f32[16]{0:T(128)S(1)}, u32[]{:S(2)}, u32[]{:S(2)}) collective-permute-start(f32[16]{0:T(128)S(1)} %get-tuple-element.12), channel_id=1, source_target_pairs={{0,3},{1,4},{2,5},{3,6},{4,7},{5,8},{6,9},{7,10},{8,11},{9,12},{10... | collective-permute-start | bytes 200 | tf_op jit(solution)/shard_map/ppermute | solution.py:12
  22.8 3.0 %collective-permute-start = (f32[16]{0:T(128)S(1)}, f32[16]{0:T(128)S(1)}, u32[]{:S(2)}, u32[]{:S(2)}) collective-permute-start(f32[16]{0:T(128)S(1)} %get-tuple-element.17), channel_id=1, source_target_pairs={{0,29},{1,30},{2,31},{3,0},{4,1},{5,2},{6,3},{7,4},{8,5},{9,6},{10... | collective-permute-start | bytes 200 | tf_op jit(solution)/shard_map/ppermute | solution.py:12
  25.8 1.4 %fusion.20 = f32[48,48,256]{2,0,1:T(8,128)S(1)} fusion(f32[16,48,256]{2,1,0:T(8,128)S(1)} %get-tuple-element.11, f32[16]{0:T(128)S(1)} %get-tuple-element.18), kind=kOutput, calls=%fused_computation.27 | convolution fusion | flops 113246976 | bytes 3145792 | tf_op jit(solution)/shard_map/kj,kfr->jfr/dot_general | solution.py:19
  27.3 28.8 %collective-permute-done = f32[16]{0:T(128)S(1)} collective-permute-done((f32[16]{0:T(128)S(1)}, f32[16]{0:T(128)S(1)}, u32[]{:S(2)}, u32[]{:S(2)}) %collective-permute-start) | collective-permute-done | bytes 96 | tf_op jit(solution)/shard_map/ppermute | solution.py:12
  56.1 5.6 %collective-permute-start.2 = (f32[16]{0:T(128)S(1)}, f32[16]{0:T(128)S(1)}, u32[]{:S(2)}, u32[]{:S(2)}) collective-permute-start(f32[16]{0:T(128)S(1)} %get-tuple-element.16), channel_id=1, source_target_pairs={{0,30},{1,31},{2,0},{3,1},{4,2},{5,3},{6,4},{7,5},{8,6},{9,7},{10,... | collective-permute-start | bytes 200 | tf_op jit(solution)/shard_map/ppermute | solution.py:12
  61.6 15.5 %collective-permute-start.7 = (f32[16,48,256]{2,1,0:T(8,128)S(1)}, f32[16,48,256]{2,1,0:T(8,128)S(1)}, u32[]{:S(2)}, u32[]{:S(2)}) collective-permute-start(f32[16,48,256]{2,1,0:T(8,128)S(1)} %get-tuple-element.7), channel_id=1, source_target_pairs={{0,1},{1,2},{2,3},{3,4},{4,5},{5,6},{6,7},{7,8},{8,9},{9,10},{10,1... | collective-permute-start | bytes 2359304 | tf_op jit(solution)/shard_map/ppermute | solution.py:12
  77.1 1.4 %fusion.18 = f32[48,48,256]{2,0,1:T(8,128)S(1)} fusion(f32[16,48,256]{2,1,0:T(8,128)S(1)} %collective-permute-done.1, f32[16]{0:T(128)S(1)} %collective-permute-done), kind=kOutput, calls=%fused_computation.25 | convolution fusion | flops 113246976 | bytes 3145792 | tf_op jit(solution)/shard_map/kj,kfr->jfr/dot_general | solution.py:19
  78.6 4.5 %collective-permute-start.4 = (f32[16]{0:T(128)S(1)}, f32[16]{0:T(128)S(1)}, u32[]{:S(2)}, u32[]{:S(2)}) collective-permute-start(f32[16]{0:T(128)S(1)} %get-tuple-element.15), channel_id=1, source_target_pairs={{0,31},{1,0},{2,1},{3,2},{4,3},{5,4},{6,5},{7,6},{8,7},{9,8},{10,9... | collective-permute-start | bytes 200 | tf_op jit(solution)/shard_map/ppermute | solution.py:12
  83.1 1.4 %fusion.16 = f32[48,48,256]{2,0,1:T(8,128)S(1)} fusion(f32[16,48,256]{2,1,0:T(8,128)S(1)} %collective-permute-done.3, f32[16]{0:T(128)S(1)} %collective-permute-done.2), kind=kOutput, calls=%fused_computation.23 | convolution fusion | flops 113246976 | bytes 3145792 | tf_op jit(solution)/shard_map/kj,kfr->jfr/dot_general | solution.py:19
  84.6 0.2 collective-permute-start.11
  84.8 1.4 %fusion.14 = f32[48,48,256]{2,0,1:T(8,128)S(1)} fusion(f32[16,48,256]{2,1,0:T(8,128)S(1)} %collective-permute-done.5, f32[16]{0:T(128)S(1)} %collective-permute-done.4), kind=kOutput, calls=%fused_computation.21 | convolution fusion | flops 113246976 | bytes 3145792 | tf_op jit(solution)/shard_map/kj,kfr->jfr/dot_general | solution.py:19
  86.3 13.9 %collective-permute-done.6 = f32[16]{0:T(128)S(1)} collective-permute-done((f32[16]{0:T(128)S(1)}, f32[16]{0:T(128)S(1)}, u32[]{:S(2)}, u32[]{:S(2)}) %collective-permute-start.6) | collective-permute-done | bytes 96 | tf_op jit(solution)/shard_map/ppermute | solution.py:12
  100.2 7.0 %collective-permute-start.8 = (f32[16]{0:T(128)S(1)}, f32[16]{0:T(128)S(1)}, u32[]{:S(2)}, u32[]{:S(2)}) collective-permute-start(f32[16]{0:T(128)S(1)} %get-tuple-element.13), channel_id=1, source_target_pairs={{0,2},{1,3},{2,4},{3,5},{4,6},{5,7},{6,8},{7,9},{8,10},{9,11},{10,... | collective-permute-start | bytes 200 | tf_op jit(solution)/shard_map/ppermute | solution.py:12
  107.2 1.4 %fusion.12 = f32[48,48,256]{2,0,1:T(8,128)S(1)} fusion(f32[16,48,256]{2,1,0:T(8,128)S(1)} %collective-permute-done.7, f32[16]{0:T(128)S(1)} %collective-permute-done.6), kind=kOutput, calls=%fused_computation.19 | convolution fusion | flops 113246976 | bytes 3145792 | tf_op jit(solution)/shard_map/kj,kfr->jfr/dot_general | solution.py:19
  108.6 11.9 %collective-permute-done.8 = f32[16]{0:T(128)S(1)} collective-permute-done((f32[16]{0:T(128)S(1)}, f32[16]{0:T(128)S(1)}, u32[]{:S(2)}, u32[]{:S(2)}) %collective-permute-start.8) | collective-permute-done | bytes 96 | tf_op jit(solution)/shard_map/ppermute | solution.py:12
  120.5 1.4 %fusion.10 = f32[48,48,256]{2,0,1:T(8,128)S(1)} fusion(f32[16,48,256]{2,1,0:T(8,128)S(1)} %collective-permute-done.9, f32[16]{0:T(128)S(1)} %collective-permute-done.8), kind=kOutput, calls=%fused_computation.17 | convolution fusion | flops 113246976 | bytes 3145792 | tf_op jit(solution)/shard_map/kj,kfr->jfr/dot_general | solution.py:19
  122.0 6.9 %collective-permute-done.11 = f32[16,48,256]{2,1,0:T(8,128)S(1)} collective-permute-done((f32[16,48,256]{2,1,0:T(8,128)S(1)}, f32[16,48,256]{2,1,0:T(8,128)S(1)}, u32[]{:S(2)}, u32[]{:S(2)}) %collective-permute-start.11) | collective-permute-done | bytes 786464 | tf_op jit(solution)/shard_map/ppermute | solution.py:12
  128.9 3.4 %add_bitcast_fusion = f32[48,48,256]{2,1,0:T(8,128)} fusion(f32[48,48,256]{2,0,1:T(8,128)S(1)} %fusion.10, f32[48,48,256]{2,0,1:T(8,128)S(1)} %fusion.12, f32[48,48,256]{2,0,1:T(8,128)S(1)} %fusion.14, f32[48,48,256]{2,0,1:T(8,128)S(1)} %fusion.16, f32[48,48,256]{2,0,1:T(8,128)S(1)} %fusion.20, f32[48,48,256]{2,0,1:T(8,128)S(1)} %fusion.18, ...), kind=kOutput, calls=%fused_computation.5 | convolution fusion | flops 116785920 | bytes 17301568 | tf_op jit(solution)/shard_map/kj,kfr->jfr/dot_general | solution.py:19
  132.3 1.9 %reshape.94 = f32[4,12,12288]{2,1,0:T(8,128)S(1)} reshape(f32[48,48,256]{2,1,0:T(8,128)} %add_bitcast_fusion) | data formatting | bytes 4718592 | tf_op jit(solution)/shard_map/reshape | solution.py:53
  134.2 2.9 %copy.23 = f32[4,12,12288]{2,0,1:T(4,128)} copy(f32[4,12,12288]{2,1,0:T(8,128)S(1)} %reshape.94) | data formatting | bytes 4718592 | tf_op jit(solution)/shard_map/reshape | solution.py:53
  (17 shorter events, 0.1 us)
Async XLA Ops:
  13.8 7.5 %copy-start = (s32[1,7,16]{2,0,1:T(1,128)S(1)}, s32[1,7,16]{2,0,1:T(1,128)}, u32[]{:S(2)}) copy-start(s32[1,7,16]{2,0,1:T(1,128)} %param.9) | copy-start | bytes 1348
  14.2 47.4 %collective-permute-start.1 = (f32[16,48,256]{2,1,0:T(8,128)S(1)}, f32[16,48,256]{2,1,0:T(8,128)S(1)}, u32[]{:S(2)}, u32[]{:S(2)}) collective-permute-start(f32[16,48,256]{2,1,0:T(8,128)S(1)} %get-tuple-element.10), channel_id=1, source_target_pairs={{0,29},{1,30},{2,31},{3,0},{4,1},{5,2},{6,3},{7,4},{8,5},{9,6},{10... | collective-permute-start | bytes 2359304 | tf_op jit(solution)/shard_map/ppermute | solution.py:12
  19.7 63.4 %collective-permute-start.3 = (f32[16,48,256]{2,1,0:T(8,128)S(1)}, f32[16,48,256]{2,1,0:T(8,128)S(1)}, u32[]{:S(2)}, u32[]{:S(2)}) collective-permute-start(f32[16,48,256]{2,1,0:T(8,128)S(1)} %get-tuple-element.9), channel_id=1, source_target_pairs={{0,30},{1,31},{2,0},{3,1},{4,2},{5,3},{6,4},{7,5},{8,6},{9,7},{10,... | collective-permute-start | bytes 2359304 | tf_op jit(solution)/shard_map/ppermute | solution.py:12
  21.3 100.7 %collective-permute-start.10 = (f32[16]{0:T(128)S(1)}, f32[16]{0:T(128)S(1)}, u32[]{:S(2)}, u32[]{:S(2)}) collective-permute-start(f32[16]{0:T(128)S(1)} %get-tuple-element.12), channel_id=1, source_target_pairs={{0,3},{1,4},{2,5},{3,6},{4,7},{5,8},{6,9},{7,10},{8,11},{9,12},{10... | collective-permute-start | bytes 200 | tf_op jit(solution)/shard_map/ppermute | solution.py:12
  22.8 33.3 %collective-permute-start = (f32[16]{0:T(128)S(1)}, f32[16]{0:T(128)S(1)}, u32[]{:S(2)}, u32[]{:S(2)}) collective-permute-start(f32[16]{0:T(128)S(1)} %get-tuple-element.17), channel_id=1, source_target_pairs={{0,29},{1,30},{2,31},{3,0},{4,1},{5,2},{6,3},{7,4},{8,5},{9,6},{10... | collective-permute-start | bytes 200 | tf_op jit(solution)/shard_map/ppermute | solution.py:12
  25.8 58.8 %collective-permute-start.5 = (f32[16,48,256]{2,1,0:T(8,128)S(1)}, f32[16,48,256]{2,1,0:T(8,128)S(1)}, u32[]{:S(2)}, u32[]{:S(2)}) collective-permute-start(f32[16,48,256]{2,1,0:T(8,128)S(1)} %get-tuple-element.8), channel_id=1, source_target_pairs={{0,31},{1,0},{2,1},{3,2},{4,3},{5,4},{6,5},{7,6},{8,7},{9,8},{10,9... | collective-permute-start | bytes 2359304 | tf_op jit(solution)/shard_map/ppermute | solution.py:12
  56.1 22.5 %collective-permute-start.2 = (f32[16]{0:T(128)S(1)}, f32[16]{0:T(128)S(1)}, u32[]{:S(2)}, u32[]{:S(2)}) collective-permute-start(f32[16]{0:T(128)S(1)} %get-tuple-element.16), channel_id=1, source_target_pairs={{0,30},{1,31},{2,0},{3,1},{4,2},{5,3},{6,4},{7,5},{8,6},{9,7},{10,... | collective-permute-start | bytes 200 | tf_op jit(solution)/shard_map/ppermute | solution.py:12
  61.6 45.5 %collective-permute-start.7 = (f32[16,48,256]{2,1,0:T(8,128)S(1)}, f32[16,48,256]{2,1,0:T(8,128)S(1)}, u32[]{:S(2)}, u32[]{:S(2)}) collective-permute-start(f32[16,48,256]{2,1,0:T(8,128)S(1)} %get-tuple-element.7), channel_id=1, source_target_pairs={{0,1},{1,2},{2,3},{3,4},{4,5},{5,6},{6,7},{7,8},{8,9},{9,10},{10,1... | collective-permute-start | bytes 2359304 | tf_op jit(solution)/shard_map/ppermute | solution.py:12
  78.6 5.9 %collective-permute-start.4 = (f32[16]{0:T(128)S(1)}, f32[16]{0:T(128)S(1)}, u32[]{:S(2)}, u32[]{:S(2)}) collective-permute-start(f32[16]{0:T(128)S(1)} %get-tuple-element.15), channel_id=1, source_target_pairs={{0,31},{1,0},{2,1},{3,2},{4,3},{5,4},{6,5},{7,6},{8,7},{9,8},{10,9... | collective-permute-start | bytes 200 | tf_op jit(solution)/shard_map/ppermute | solution.py:12
  83.1 37.5 %collective-permute-start.9 = (f32[16,48,256]{2,1,0:T(8,128)S(1)}, f32[16,48,256]{2,1,0:T(8,128)S(1)}, u32[]{:S(2)}, u32[]{:S(2)}) collective-permute-start(f32[16,48,256]{2,1,0:T(8,128)S(1)} %get-tuple-element.6), channel_id=1, source_target_pairs={{0,2},{1,3},{2,4},{3,5},{4,6},{5,7},{6,8},{7,9},{8,10},{9,11},{10,... | collective-permute-start | bytes 2359304 | tf_op jit(solution)/shard_map/ppermute | solution.py:12
  84.5 15.7 %collective-permute-start.6 = (f32[16]{0:T(128)S(1)}, f32[16]{0:T(128)S(1)}, u32[]{:S(2)}, u32[]{:S(2)}) collective-permute-start(f32[16]{0:T(128)S(1)} %get-tuple-element.14), channel_id=1, source_target_pairs={{0,1},{1,2},{2,3},{3,4},{4,5},{5,6},{6,7},{7,8},{8,9},{9,10},{10,1... | collective-permute-start | bytes 200 | tf_op jit(solution)/shard_map/ppermute | solution.py:12
  84.6 44.3 %collective-permute-start.11 = (f32[16,48,256]{2,1,0:T(8,128)S(1)}, f32[16,48,256]{2,1,0:T(8,128)S(1)}, u32[]{:S(2)}, u32[]{:S(2)}) collective-permute-start(f32[16,48,256]{2,1,0:T(8,128)S(1)} %get-tuple-element.5), channel_id=1, source_target_pairs={{0,3},{1,4},{2,5},{3,6},{4,7},{5,8},{6,9},{7,10},{8,11},{9,12},{10... | collective-permute-start | bytes 2359304 | tf_op jit(solution)/shard_map/ppermute | solution.py:12
  100.2 20.4 %collective-permute-start.8 = (f32[16]{0:T(128)S(1)}, f32[16]{0:T(128)S(1)}, u32[]{:S(2)}, u32[]{:S(2)}) collective-permute-start(f32[16]{0:T(128)S(1)} %get-tuple-element.13), channel_id=1, source_target_pairs={{0,2},{1,3},{2,4},{3,5},{4,6},{5,7},{6,8},{7,9},{8,10},{9,11},{10,... | collective-permute-start | bytes 200 | tf_op jit(solution)/shard_map/ppermute | solution.py:12
where the time goes:
time: 137 us
  waiting for transfers between devices  61.6 us (45%)
  starting transfers between devices  44.4 us (32%)
  matrix products  17.8 us (13%)
  other arithmetic  6.87 us (5%)
  local copies, waits for them, and re-layouts  6.33 us (5%)
    ppermute x12, waiting for transfers between devices, shifted(): return lax.ppermute(value, axis, pairs)  61.6 us
    ppermute x12, starting transfers between devices, shifted(): return lax.ppermute(value, axis, pairs)  44.4 us
    dot_general x7, matrix products, settle(): jnp.einsum('kj,kfr->jfr', onehot, partial_value, precision=lax.Precision....  12 us
    dot_general x1, matrix products, on_device(): jnp.einsum('okrc,fokc->okfr', weights[0], picked, preferred_element_type=...  5.81 us
    reshape x2, local copies, waits for them, and re-layouts, on_device(): totals.transpose(1, 0, 2).reshape(num_steps, num_kinds, AB_DEV * block_rows)  4.82 us
    reduce_sum x1, other arithmetic, on_device(): jnp.sum(tile_flux.astype(jnp.float32) * tile_frac[None, None], axis=2)  3.97 us
  transfers between devices with their start and end apart: 12, of which 4 were waited for; matrix products, arithmetic and copies ran while one was open for 6% of the time, Pallas kernels for 0%

commit v1 on v0

v1 whole, which is shorter than its diff:
```python
import functools

import jax
import jax.numpy as jnp
from jax import lax
from jax.experimental import pallas as pl
from jax.experimental.pallas import tpu as pltpu
from jax.sharding import PartitionSpec as P

CHUNKS = 2


def send_order(num_off, reach):
    order = []
    for away in range(reach, 0, -1):
        order += [reach + away, reach - away]
    return order + [reach]


def exchange_kernel(axes, sizes, merged_ref, col_ref, count_ref, rows_ref, weights_ref,
                    arrived_ref, arrived_rows_ref,
                    weights_buf, part_buf, weight_sem, own_sem, send_sem, recv_sem,
                    row_send_sem, row_recv_sem):
    num_off, slots = weights_buf.shape[0], weights_buf.shape[1]
    reach = num_off // 2
    inner = sizes[1]
    count = sizes[0] * sizes[1]
    me = lax.axis_index(axes[0]) * inner + lax.axis_index(axes[1])
    order = send_order(num_off, reach)
    step = slots // CHUNKS

    def place(offset):
        there = lax.rem(me + offset - reach + count, count)
        return (there // inner, lax.rem(there, inner))

    loads = {}
    for offset in order:
        loads[offset] = pltpu.make_async_copy(
            weights_ref.at[offset], weights_buf.at[offset], weight_sem.at[offset])
        loads[offset].start()

    barrier = pltpu.get_barrier_semaphore()
    for offset in order[:-1]:
        pl.semaphore_signal(barrier, inc=1, device_id=place(offset),
                            device_id_type=pl.DeviceIdType.MESH)
    pl.semaphore_wait(barrier, num_off - 1)

    copies = []
    for offset in order:
        loads[offset].wait()
        if offset != reach:
            row_copy = pltpu.make_async_remote_copy(
                src_ref=rows_ref.at[offset], dst_ref=arrived_rows_ref.at[offset],
                send_sem=row_send_sem.at[offset], recv_sem=row_recv_sem.at[offset],
                device_id=place(offset), device_id_type=pl.DeviceIdType.MESH)
            row_copy.start()
            copies.append(row_copy)
        for chunk in range(CHUNKS):
            def one_slot(slot, carry, offset=offset):
                live = jnp.where(slot < count_ref[0, offset], 1.0, 0.0).astype(jnp.float32)
                picked = merged_ref[col_ref[0, offset, slot]]
                value = lax.dot_general(picked, weights_buf[offset, slot],
                                        (((1,), (1,)), ((), ())),
                                        preferred_element_type=jnp.float32)
                part_buf[offset, slot] = value * live
                return carry

            lax.fori_loop(chunk * step, (chunk + 1) * step, one_slot, 0)
            span = pl.ds(chunk * step, step)
            if offset != reach:
                copy = pltpu.make_async_remote_copy(
                    src_ref=part_buf.at[offset, span], dst_ref=arrived_ref.at[offset, span],
                    send_sem=send_sem.at[offset, chunk], recv_sem=recv_sem.at[offset, chunk],
                    device_id=place(offset), device_id_type=pl.DeviceIdType.MESH)
            else:
                copy = pltpu.make_async_copy(
                    part_buf.at[offset, span], arrived_ref.at[offset, span], own_sem.at[chunk])
            copy.start()
            copies.append(copy)
    own_rows = pltpu.make_async_copy(rows_ref.at[reach], arrived_rows_ref.at[reach],
                                     own_sem.at[CHUNKS])
    own_rows.start()
    copies.append(own_rows)
    for copy in copies:
        copy.wait()


def settle_kernel(rows_ref, arrived_ref, out_ref, arrived_buf, total, load_sem):
    num_off, slots = arrived_buf.shape[0], arrived_buf.shape[1]
    num_steps, num_kinds = out_ref.shape[0], out_ref.shape[1]
    blocks, block_rows = total.shape[0], total.shape[2]
    loads = []
    for offset in range(num_off):
        load = pltpu.make_async_copy(
            arrived_ref.at[offset], arrived_buf.at[offset], load_sem.at[offset])
        load.start()
        loads.append(load)
    total[...] = jnp.zeros_like(total)
    for offset in range(num_off):
        loads[offset].wait()

        def one_slot(slot, carry, offset=offset):
            row = rows_ref[offset, 0, slot]
            total[row] = total[row] + arrived_buf[offset, slot]
            return carry

        lax.fori_loop(0, slots, one_slot, 0)

    def one_block(block, carry):
        lanes = pl.ds(pl.multiple_of(block * block_rows, block_rows), block_rows)
        for step in range(num_steps):
            out_ref[step, :, lanes] = total[block, pl.ds(step * num_kinds, num_kinds), :]
        return carry

    lax.fori_loop(0, blocks, one_block, 0)


def on_device(axes, sizes, atm_blocks, tile_flux, tile_frac, weights, block_row, block_col,
              send_counts):
    num_steps, num_kinds = tile_flux.shape[0], tile_flux.shape[1]
    num_flux = num_steps * num_kinds
    num_off, slots, block_rows, block_cols = weights.shape[1:]
    frac_sum = jnp.sum(tile_frac, axis=0)
    merged = (
        jnp.sum(tile_flux.astype(jnp.float32) * tile_frac[None, None], axis=2) / frac_sum
    ).astype(jnp.bfloat16)
    land_blocks = merged.reshape(num_flux, -1, block_cols).transpose(1, 0, 2)
    rows = jnp.pad(block_row[0], ((0, 0), (0, 128 - slots))).reshape(num_off, 1, 128)

    smem = pl.BlockSpec(memory_space=pltpu.SMEM)
    vmem = pl.BlockSpec(memory_space=pltpu.VMEM)
    anywhere = pl.BlockSpec(memory_space=pl.ANY)
    arrived, arrived_rows = pl.pallas_call(
        functools.partial(exchange_kernel, axes, sizes),
        out_shape=(
            jax.ShapeDtypeStruct((num_off, slots, num_flux, block_rows), jnp.float32),
            jax.ShapeDtypeStruct((num_off, 1, 128), jnp.int32),
        ),
        in_specs=[vmem, smem, smem, anywhere, anywhere],
        out_specs=(anywhere, anywhere),
        scratch_shapes=[
            pltpu.VMEM(weights.shape[1:], weights.dtype),
            pltpu.VMEM((num_off, slots, num_flux, block_rows), jnp.float32),
            pltpu.SemaphoreType.DMA((num_off,)),
            pltpu.SemaphoreType.DMA((CHUNKS + 1,)),
            pltpu.SemaphoreType.DMA((num_off, CHUNKS)),
            pltpu.SemaphoreType.DMA((num_off, CHUNKS)),
            pltpu.SemaphoreType.DMA((num_off,)),
            pltpu.SemaphoreType.DMA((num_off,)),
        ],
        compiler_params=pltpu.CompilerParams(collective_id=0, has_side_effects=True),
        name="exchange",
    )(land_blocks, block_col, send_counts, rows, weights[0])

    return pl.pallas_call(
        settle_kernel,
        out_shape=jax.ShapeDtypeStruct((num_steps, num_kinds, atm_blocks * block_rows),
                                       jnp.float32),
        in_specs=[smem, anywhere],
        out_specs=vmem,
        scratch_shapes=[
            pltpu.VMEM((num_off, slots, num_flux, block_rows), jnp.float32),
            pltpu.VMEM((atm_blocks, num_flux, block_rows), jnp.float32),
            pltpu.SemaphoreType.DMA((num_off,)),
        ],
        name="settle",
    )(arrived_rows, arrived)


AB_DEV = 48


def solution(mesh):
    axes = ("gx", "gy")
    sizes = (mesh.shape["gx"], mesh.shape["gy"])
    return jax.shard_map(
        functools.partial(on_device, axes, sizes, AB_DEV),
        mesh=mesh,
        in_specs=(
            P(None, None, None, ("gx", "gy")),
            P(None, ("gx", "gy")),
            P(("gx", "gy"), None, None, None, None),
            P(("gx", "gy"), None, None),
            P(("gx", "gy"), None, None),
            P(("gx", "gy"), None),
        ),
        out_specs=P(None, None, ("gx", "gy")),
        check_vma=False,
    )
```

time: 137 us -> 128 us (0.934)
  the two profiles are of different devices: /device:TPU:0 before, /device:TPU:9 now
where the time goes in v1:
time: 128 us
  Pallas kernels  114 us (89%)
  local copies, waits for them, and re-layouts  7.57 us (6%)
  other arithmetic  6.12 us (5%)
    pallas_call x1, Pallas kernels, on_device(): pl.pallas_call(functools.partial(exchange_kernel, axes, sizes), out_shape...  108 us
    pallas_call x1, Pallas kernels, on_device(): pl.pallas_call(settle_kernel, out_shape=jax.ShapeDtypeStruct((num_steps,...  5.71 us
    pallas_call x1, local copies, waits for them, and re-layouts, on_device(): pl.pallas_call(settle_kernel, out_shape=jax.ShapeDtypeStruct((num_steps,...  4.81 us
    reduce_sum x1, other arithmetic, on_device(): jnp.sum(tile_flux.astype(jnp.float32) * tile_frac[None, None], axis=2)  3.97 us

profile of v1, /device:TPU:9, one launch (start us, length us, event | category | flops | bytes accessed | tf_op | source)
XLA Modules:
  0.0 127.6 jit_solution(1043875853435750534)
XLA Ops:
  0.0 0.7 copy.19
  0.7 0.6 reshape.9.rows_ref
  1.3 1.3 %copy.10.col_ref = s32[1,7,16]{2,1,0:T(8,128)} copy(s32[1,7,16]{2,0,1:T(1,128)} %param.10) | data formatting | bytes 896 | tf_op args[4]
  2.6 0.9 reduce_sum.22
  3.5 4.0 %multiply_reduce_fusion = f32[4,12,4096]{2,1,0:T(8,128)S(1)} fusion(bf16[4,12,8,4096]{3,2,1,0:T(8,128)(2,1)} %param.6, f32[8,4096]{1,0:T(8,128)} %param.7), kind=kLoop, calls=%fused_computation | loop fusion | flops 4521984 | bytes 4063232 | tf_op jit(solution)/shard_map/reduce_sum | solution.py:125
  7.5 0.2 reduce_sum.21
  7.7 1.2 fusion.1.merged_ref
  8.9 108.2 %exchange.1 = (f32[7,16,48,256]{3,2,1,0:T(8,128)}, s32[7,1,128]{2,1,0:T(1,128)}) custom-call(bf16[32,48,128]{2,1,0:T(8,128)(2,1)} %fusion.1.merged_ref, s32[1,7,16]{2,1,0:T(8,128)} %copy.10.col_ref, s32[1,7]{1,0:T(1,128)} %count_ref.1, s32[7,1,128]{2,1,0:T(1,128)} %reshape.9.rows_ref, bf16[7,16,256,128]{3,2,1,0:T(8,128)(2,1)} %bitcast.7), custom_call_target="tpu_custom_call" | custom-call | tf_op jit(solution)/shard_map/exchange/pallas_call | solution.py:133
  117.1 5.7 %settle.1 = f32[4,12,12288]{2,1,0:T(8,128)} custom-call(s32[7,1,128]{2,1,0:T(1,128)} %get-tuple-element.7.rows_ref, f32[7,16,48,256]{3,2,1,0:T(8,128)} %get-tuple-element.8.arrived_ref), custom_call_target="tpu_custom_call" | custom-call | tf_op jit(solution)/shard_map/settle/pallas_call | solution.py:155
  122.8 4.8 %copy.11 = f32[4,12,12288]{2,0,1:T(4,128)} copy(f32[4,12,12288]{2,1,0:T(8,128)} %settle.1) | data formatting | bytes 4718592 | tf_op jit(solution)/shard_map/settle/pallas_call | solution.py:155
  (1 shorter events, 0.0 us)

commit v2 on v1

v2 whole, which is shorter than its diff:
```python
import functools

import jax
import jax.numpy as jnp
from jax import lax
from jax.experimental import pallas as pl
from jax.experimental.pallas import tpu as pltpu
from jax.sharding import PartitionSpec as P

CUTS = 8
OUT_CUTS = 4


def chunk_spans(slots):
    spans, begin, size = [], 0, max(slots // CUTS, 1)
    while begin < slots:
        size = min(size if begin == 0 else begin, slots - begin)
        spans.append((begin, size))
        begin += size
    return spans


def send_order(reach, spans):
    order = []
    for away in range(reach, 0, -1):
        for chunk in range(len(spans)):
            order += [(reach + away, chunk), (reach - away, chunk)]
    return order + [(reach, chunk) for chunk in range(len(spans))]


def exchange_kernel(axes, sizes, spans, flux_ref, frac_ref, col_ref, count_ref, rows_ref,
                    weights_ref, arrived_ref, arrived_rows_ref,
                    flux_buf, frac_buf, weights_buf, part_buf, flux_sem, frac_sem, weight_sem,
                    own_sem, send_sem, recv_sem, row_send_sem, row_recv_sem):
    num_off, slots = weights_buf.shape[0], weights_buf.shape[1]
    num_steps, num_kinds, tiles, _ = flux_ref.shape
    cols = weights_buf.shape[3]
    reach = num_off // 2
    inner = sizes[1]
    count = sizes[0] * sizes[1]
    me = lax.axis_index(axes[0]) * inner + lax.axis_index(axes[1])
    order = send_order(reach, spans)

    def place(offset):
        there = lax.rem(me + offset - reach + count, count)
        return (there // inner, lax.rem(there, inner))

    land_loads = []
    for block in range(flux_buf.shape[0]):
        lanes = pl.ds(block * cols, cols)
        land_loads.append(pltpu.make_async_copy(
            flux_ref.at[:, :, :, lanes], flux_buf.at[block], flux_sem.at[block]))
        land_loads.append(pltpu.make_async_copy(
            frac_ref.at[:, lanes], frac_buf.at[block], frac_sem.at[block]))
    for load in land_loads:
        load.start()
    loads = {}
    for offset, chunk in order:
        if offset not in loads:
            loads[offset] = pltpu.make_async_copy(
                weights_ref.at[offset], weights_buf.at[offset], weight_sem.at[offset])
            loads[offset].start()

    barrier = pltpu.get_barrier_semaphore()
    for offset in range(num_off):
        if offset != reach:
            pl.semaphore_signal(barrier, inc=1, device_id=place(offset),
                                device_id_type=pl.DeviceIdType.MESH)
    pl.semaphore_wait(barrier, num_off - 1)

    for load in land_loads:
        load.wait()
    copies = []
    loaded = set()
    for offset, chunk in order:
        begin, size = spans[chunk]
        if offset not in loaded:
            loads[offset].wait()
            loaded.add(offset)

        def one_slot(slot, carry, offset=offset):
            live = jnp.where(slot < count_ref[0, offset], 1.0, 0.0).astype(jnp.float32)
            block = col_ref[offset, 0, slot]
            frac = frac_buf[block]
            flux = flux_buf[block].astype(jnp.float32)
            flux = jnp.stack([flux[step] for step in range(num_steps)], axis=1)
            flux = flux.reshape(num_steps * num_kinds, tiles, cols)
            merged = jnp.sum(flux * frac[None], axis=1) / jnp.sum(frac, axis=0, keepdims=True)
            value = lax.dot_general(merged.astype(jnp.bfloat16), weights_buf[offset, slot],
                                    (((1,), (1,)), ((), ())),
                                    preferred_element_type=jnp.float32)
            part_buf[offset, slot] = value * live
            return carry

        lax.fori_loop(begin, begin + size, one_slot, 0)
        span = pl.ds(begin, size)
        if offset != reach:
            copy = pltpu.make_async_remote_copy(
                src_ref=part_buf.at[offset, span], dst_ref=arrived_ref.at[offset, span],
                send_sem=send_sem.at[offset, chunk], recv_sem=recv_sem.at[offset, chunk],
                device_id=place(offset), device_id_type=pl.DeviceIdType.MESH)
        else:
            copy = pltpu.make_async_copy(
                part_buf.at[offset, span], arrived_ref.at[offset, span], own_sem.at[chunk])
        copy.start()
        copies.append(copy)
        if chunk == 0:
            if offset != reach:
                copy = pltpu.make_async_remote_copy(
                    src_ref=rows_ref.at[offset], dst_ref=arrived_rows_ref.at[offset],
                    send_sem=row_send_sem.at[offset], recv_sem=row_recv_sem.at[offset],
                    device_id=place(offset), device_id_type=pl.DeviceIdType.MESH)
            else:
                copy = pltpu.make_async_copy(
                    rows_ref.at[reach], arrived_rows_ref.at[reach], own_sem.at[len(spans)])
            copy.start()
            copies.append(copy)
    for copy in copies:
        copy.wait()


def settle_kernel(rows_ref, arrived_ref, out_ref, arrived_buf, total, out_buf, load_sem,
                  out_sem):
    num_off, slots = arrived_buf.shape[0], arrived_buf.shape[1]
    num_kinds, num_steps = out_ref.shape[0], out_ref.shape[1]
    blocks, _, block_rows = total.shape
    loads = []
    for offset in range(num_off):
        load = pltpu.make_async_copy(
            arrived_ref.at[offset], arrived_buf.at[offset], load_sem.at[offset])
        load.start()
        loads.append(load)
    total[...] = jnp.zeros_like(total)
    for offset in range(num_off):
        loads[offset].wait()

        def one_slot(slot, carry, offset=offset):
            row = rows_ref[offset, 0, slot]
            total[row] = total[row] + arrived_buf[offset, slot]
            return carry

        lax.fori_loop(0, slots, one_slot, 0, unroll=4)

    per_cut = blocks // OUT_CUTS
    stores = []
    for cut in range(OUT_CUTS):
        def one_block(block, carry):
            lanes = pl.ds(pl.multiple_of(block * block_rows, block_rows), block_rows)
            out_buf[:, :, lanes] = total[block].reshape(num_kinds, num_steps, block_rows)
            return carry

        lax.fori_loop(cut * per_cut, (cut + 1) * per_cut, one_block, 0, unroll=2)
        lanes = pl.ds(cut * per_cut * block_rows, per_cut * block_rows)
        store = pltpu.make_async_copy(
            out_buf.at[:, :, lanes], out_ref.at[:, :, lanes], out_sem.at[cut])
        store.start()
        stores.append(store)
    for store in stores:
        store.wait()


def on_device(axes, sizes, atm_blocks, tile_flux, tile_frac, weights, block_row, block_col,
              send_counts):
    num_steps, num_kinds = tile_flux.shape[0], tile_flux.shape[1]
    num_flux = num_steps * num_kinds
    num_off, slots, block_rows, block_cols = weights.shape[1:]
    tiles = tile_flux.shape[2]
    land_blocks = tile_flux.shape[3] // block_cols
    spans = chunk_spans(slots)
    rows = block_row.transpose(1, 0, 2)
    columns = block_col.transpose(1, 0, 2)

    smem = pl.BlockSpec(memory_space=pltpu.SMEM)
    anywhere = pl.BlockSpec(memory_space=pl.ANY)
    arrived, arrived_rows = pl.pallas_call(
        functools.partial(exchange_kernel, axes, sizes, spans),
        out_shape=(
            jax.ShapeDtypeStruct((num_off, slots, num_flux, block_rows), jnp.float32),
            jax.ShapeDtypeStruct(rows.shape, jnp.int32),
        ),
        in_specs=[anywhere, anywhere, smem, smem, anywhere, anywhere],
        out_specs=(anywhere, anywhere),
        scratch_shapes=[
            pltpu.VMEM((land_blocks, num_steps, num_kinds, tiles, block_cols), tile_flux.dtype),
            pltpu.VMEM((land_blocks, tiles, block_cols), tile_frac.dtype),
            pltpu.VMEM(weights.shape[1:], weights.dtype),
            pltpu.VMEM((num_off, slots, num_flux, block_rows), jnp.float32),
            pltpu.SemaphoreType.DMA((land_blocks,)),
            pltpu.SemaphoreType.DMA((land_blocks,)),
            pltpu.SemaphoreType.DMA((num_off,)),
            pltpu.SemaphoreType.DMA((len(spans) + 1,)),
            pltpu.SemaphoreType.DMA((num_off, len(spans))),
            pltpu.SemaphoreType.DMA((num_off, len(spans))),
            pltpu.SemaphoreType.DMA((num_off,)),
            pltpu.SemaphoreType.DMA((num_off,)),
        ],
        compiler_params=pltpu.CompilerParams(collective_id=0, has_side_effects=True),
        name="exchange",
    )(tile_flux, tile_frac, columns, send_counts, rows, weights[0])

    out = pl.pallas_call(
        settle_kernel,
        out_shape=jax.ShapeDtypeStruct((num_kinds, num_steps, atm_blocks * block_rows),
                                       jnp.float32),
        in_specs=[smem, anywhere],
        out_specs=anywhere,
        scratch_shapes=[
            pltpu.VMEM((num_off, slots, num_flux, block_rows), jnp.float32),
            pltpu.VMEM((atm_blocks, num_flux, block_rows), jnp.float32),
            pltpu.VMEM((num_kinds, num_steps, atm_blocks * block_rows), jnp.float32),
            pltpu.SemaphoreType.DMA((num_off,)),
            pltpu.SemaphoreType.DMA((OUT_CUTS,)),
        ],
        name="settle",
    )(arrived_rows, arrived)
    return out.transpose(1, 0, 2)


AB_DEV = 48


def solution(mesh):
    axes = ("gx", "gy")
    sizes = (mesh.shape["gx"], mesh.shape["gy"])
    return jax.shard_map(
        functools.partial(on_device, axes, sizes, AB_DEV),
        mesh=mesh,
        in_specs=(
            P(None, None, None, ("gx", "gy")),
            P(None, ("gx", "gy")),
            P(("gx", "gy"), None, None, None, None),
            P(("gx", "gy"), None, None),
            P(("gx", "gy"), None, None),
            P(("gx", "gy"), None),
        ),
        out_specs=P(None, None, ("gx", "gy")),
        check_vma=False,
    )
```

time: 128 us -> 115 us (0.90)
  local copies, waits for them, and re-layouts: 7.57 us -> 0 us
  other arithmetic: 6.12 us -> 0 us
    reduce_sum x2 -> x0, other arithmetic: 4.9 us -> none  [the longest x1 3.97 us: on_device(): jnp.sum(tile_flux.astype(jnp.float32) * tile_frac[None, None], axis=2)]
    pallas_call x1 -> x0, local copies, waits for them, and re-layouts: 4.81 us -> none  [on_device(): pl.pallas_call(settle_kernel, out_shape=jax.ShapeDtypeStruct((num_steps,...]
    unnamed x2 -> x0, local copies, waits for them, and re-layouts: 1.96 us -> none
where the time goes in v2:
time: 115 us
  Pallas kernels  115 us (100%)
    pallas_call x1, Pallas kernels, on_device(): pl.pallas_call(functools.partial(exchange_kernel, axes, sizes, spans), ou...  110 us
    pallas_call x1, Pallas kernels, on_device(): pl.pallas_call(settle_kernel, out_shape=jax.ShapeDtypeStruct((num_kinds,...  4.93 us

profile of v2, /device:TPU:9, one launch (start us, length us, event | category | flops | bytes accessed | tf_op | source)
XLA Modules:
  0.0 115.0 jit_solution(8503396719632630365)
XLA Ops:
  0.0 110.0 %exchange.1 = (f32[7,16,48,256]{3,2,1,0:T(8,128)}, s32[7,1,16]{2,1,0:T(1,128)}) custom-call(bf16[4,12,8,4096]{3,2,1,0:T(8,128)(2,1)} %flux_ref.1, f32[8,4096]{1,0:T(8,128)} %frac_ref.1, s32[7,1,16]{2,1,0:T(1,128)} %bitcast.5, s32[1,7]{1,0:T(1,128)} %count_ref.1, s32[7,1,16]{2,1,0:T(1,128)} %bitcast.6, bf16[7,16,256,128]{3,2,1,0:T(8,128)(2,1)} %bitcast.4), custom_call_target="tpu_custom_call" | custom-call | tf_op jit(solution)/shard_map/exchange/pallas_call | solution.py:175
  110.1 4.9 %settle.1 = f32[12,4,12288]{2,1,0:T(4,128)} custom-call(s32[7,1,16]{2,1,0:T(1,128)} %get-tuple-element.7.rows_ref, f32[7,16,48,256]{3,2,1,0:T(8,128)} %get-tuple-element.8.arrived_ref), custom_call_target="tpu_custom_call" | custom-call | tf_op jit(solution)/shard_map/settle/pallas_call | solution.py:201

commit v3 on v2

--- a/solution.py
+++ b/solution.py
@@ -44,6 +44,12 @@
     def place(offset):
         there = lax.rem(me + offset - reach + count, count)
         return (there // inner, lax.rem(there, inner))
+
+    barrier = pltpu.get_barrier_semaphore()
+    for offset in range(num_off):
+        if offset != reach:
+            pl.semaphore_signal(barrier, inc=1, device_id=place(offset),
+                                device_id_type=pl.DeviceIdType.MESH)
 
     land_loads = []
     for block in range(flux_buf.shape[0]):
@@ -61,13 +67,6 @@
                 weights_ref.at[offset], weights_buf.at[offset], weight_sem.at[offset])
             loads[offset].start()
 
-    barrier = pltpu.get_barrier_semaphore()
-    for offset in range(num_off):
-        if offset != reach:
-            pl.semaphore_signal(barrier, inc=1, device_id=place(offset),
-                                device_id_type=pl.DeviceIdType.MESH)
-    pl.semaphore_wait(barrier, num_off - 1)
-
     for load in land_loads:
         load.wait()
     copies = []
@@ -93,6 +92,8 @@
             return carry
 
         lax.fori_loop(begin, begin + size, one_slot, 0)
+        if not copies:
+            pl.semaphore_wait(barrier, num_off - 1)
         span = pl.ds(begin, size)
         if offset != reach:
             copy = pltpu.make_async_remote_copy(
@@ -119,24 +120,18 @@
         copy.wait()
 
 
-def settle_kernel(rows_ref, arrived_ref, out_ref, arrived_buf, total, out_buf, load_sem,
-                  out_sem):
-    num_off, slots = arrived_buf.shape[0], arrived_buf.shape[1]
+def settle_kernel(rows_ref, arrived_ref, out_ref, rows, total, out_buf, load_sem, out_sem):
+    num_off, slots = arrived_ref.shape[0], arrived_ref.shape[1]
     num_kinds, num_steps = out_ref.shape[0], out_ref.shape[1]
     blocks, _, block_rows = total.shape
-    loads = []
+    load = pltpu.make_async_copy(rows_ref, rows, load_sem)
+    load.start()
+    total[...] = jnp.zeros_like(total)
+    load.wait()
     for offset in range(num_off):
-        load = pltpu.make_async_copy(
-            arrived_ref.at[offset], arrived_buf.at[offset], load_sem.at[offset])
-        load.start()
-        loads.append(load)
-    total[...] = jnp.zeros_like(total)
-    for offset in range(num_off):
-        loads[offset].wait()
-
         def one_slot(slot, carry, offset=offset):
-            row = rows_ref[offset, 0, slot]
-            total[row] = total[row] + arrived_buf[offset, slot]
+            row = rows[offset, 0, slot]
+            total[row] = total[row] + arrived_ref[offset, slot]
             return carry
 
         lax.fori_loop(0, slots, one_slot, 0, unroll=4)
@@ -170,16 +165,17 @@
     rows = block_row.transpose(1, 0, 2)
     columns = block_col.transpose(1, 0, 2)
 
+    vmem = pl.BlockSpec(memory_space=pltpu.VMEM)
     smem = pl.BlockSpec(memory_space=pltpu.SMEM)
-    anywhere = pl.BlockSpec(memory_space=pl.ANY)
+    hbm = pl.BlockSpec(memory_space=pltpu.HBM)
     arrived, arrived_rows = pl.pallas_call(
         functools.partial(exchange_kernel, axes, sizes, spans),
         out_shape=(
-            jax.ShapeDtypeStruct((num_off, slots, num_flux, block_rows), jnp.float32),
-            jax.ShapeDtypeStruct(rows.shape, jnp.int32),
+            pltpu.VMEM((num_off, slots, num_flux, block_rows), jnp.float32),
+            pltpu.VMEM(rows.shape, jnp.int32),
         ),
-        in_specs=[anywhere, anywhere, smem, smem, anywhere, anywhere],
-        out_specs=(anywhere, anywhere),
+        in_specs=[hbm, hbm, smem, smem, hbm, hbm],
+        out_specs=(vmem, vmem),
         scratch_shapes=[
             pltpu.VMEM((land_blocks, num_steps, num_kinds, tiles, block_cols), tile_flux.dtype),
             pltpu.VMEM((land_blocks, tiles, block_cols), tile_frac.dtype),
@@ -194,7 +190,8 @@
             pltpu.SemaphoreType.DMA((num_off,)),
             pltpu.SemaphoreType.DMA((num_off,)),
         ],
-        compiler_params=pltpu.CompilerParams(collective_id=0, has_side_effects=True),
+        compiler_params=pltpu.CompilerParams(collective_id=0, has_side_effects=True,
+                                             vmem_limit_bytes=57 * 2**20),
         name="exchange",
     )(tile_flux, tile_frac, columns, send_counts, rows, weights[0])
 
@@ -202,15 +199,16 @@
         settle_kernel,
         out_shape=jax.ShapeDtypeStruct((num_kinds, num_steps, atm_blocks * block_rows),
                                        jnp.float32),
-        in_specs=[smem, anywhere],
-        out_specs=anywhere,
+        in_specs=[vmem, vmem],
+        out_specs=hbm,
         scratch_shapes=[
-            pltpu.VMEM((num_off, slots, num_flux, block_rows), jnp.float32),
+            pltpu.SMEM(rows.shape, jnp.int32),
             pltpu.VMEM((atm_blocks, num_flux, block_rows), jnp.float32),
             pltpu.VMEM((num_kinds, num_steps, atm_blocks * block_rows), jnp.float32),
-            pltpu.SemaphoreType.DMA((num_off,)),
+            pltpu.SemaphoreType.DMA,
             pltpu.SemaphoreType.DMA((OUT_CUTS,)),
         ],
+        compiler_params=pltpu.CompilerParams(vmem_limit_bytes=16 * 2**20),
         name="settle",
     )(arrived_rows, arrived)
     return out.transpose(1, 0, 2)

time: 115 us -> 113 us (0.983)
  Pallas kernels: 115 us -> 113 us
    pallas_call x1, Pallas kernels: 4.93 us -> 2.91 us  [on_device(): pl.pallas_call(settle_kernel, out_shape=jax.ShapeDtypeStruct((num_kinds,...]
where the time goes in v3:
time: 113 us
  Pallas kernels  113 us (100%)
    pallas_call x1, Pallas kernels, on_device(): pl.pallas_call(functools.partial(exchange_kernel, axes, sizes, spans), ou...  110 us
    pallas_call x1, Pallas kernels, on_device(): pl.pallas_call(settle_kernel, out_shape=jax.ShapeDtypeStruct((num_kinds,...  2.91 us

profile of v3, /device:TPU:9, one launch (start us, length us, event | category | flops | bytes accessed | tf_op | source)
XLA Modules:
  0.0 113.0 jit_solution(17449398969571040582)
XLA Ops:
  0.0 110.0 %exchange.1 = (f32[7,16,48,256]{3,2,1,0:T(8,128)S(1)}, s32[7,1,16]{2,1,0:T(1,128)S(1)}) custom-call(bf16[4,12,8,4096]{3,2,1,0:T(8,128)(2,1)} %flux_ref.1, f32[8,4096]{1,0:T(8,128)} %frac_ref.1, s32[7,1,16]{2,1,0:T(1,128)} %bitcast.5, s32[1,7]{1,0:T(1,128)} %count_ref.1, s32[7,1,16]{2,1,0:T(1,128)} %bitcast.6, bf16[7,16,256,128]{3,2,1,0:T(8,128)(2,1)} %bitcast.4), custom_call_target="tpu_custom_call" | custom-call | tf_op jit(solution)/shard_map/exchange/pallas_call | solution.py:171
  110.1 2.9 %settle.1 = f32[12,4,12288]{2,1,0:T(4,128)} custom-call(s32[7,1,16]{2,1,0:T(1,128)S(1)} %get-tuple-element.7.rows_ref, f32[7,16,48,256]{3,2,1,0:T(8,128)S(1)} %get-tuple-element.8.arrived_ref), custom_call_target="tpu_custom_call" | custom-call | tf_op jit(solution)/shard_map/settle/pallas_call | solution.py:198

commit v4 on v3

--- a/solution.py
+++ b/solution.py
@@ -9,6 +9,7 @@
 
 CUTS = 8
 OUT_CUTS = 4
+EARLY = 4
 
 
 def chunk_spans(slots):
@@ -62,22 +63,24 @@
         load.start()
     loads = {}
     for offset, chunk in order:
-        if offset not in loads:
-            loads[offset] = pltpu.make_async_copy(
-                weights_ref.at[offset], weights_buf.at[offset], weight_sem.at[offset])
-            loads[offset].start()
+        span = pl.ds(*spans[chunk])
+        loads[offset, chunk] = pltpu.make_async_copy(
+            weights_ref.at[offset, span], weights_buf.at[offset, span],
+            weight_sem.at[offset, chunk])
+    for key in order[:EARLY]:
+        loads[key].start()
 
     for load in land_loads:
         load.wait()
+    for key in order[EARLY:]:
+        loads[key].start()
     copies = []
-    loaded = set()
     for offset, chunk in order:
         begin, size = spans[chunk]
-        if offset not in loaded:
-            loads[offset].wait()
-            loaded.add(offset)
-
-        def one_slot(slot, carry, offset=offset):
+        loads[offset, chunk].wait()
+        part_ref = arrived_ref if offset == reach else part_buf
+
+        def one_slot(slot, carry, offset=offset, part_ref=part_ref):
             live = jnp.where(slot < count_ref[0, offset], 1.0, 0.0).astype(jnp.float32)
             block = col_ref[offset, 0, slot]
             frac = frac_buf[block]
@@ -88,7 +91,7 @@
             value = lax.dot_general(merged.astype(jnp.bfloat16), weights_buf[offset, slot],
                                     (((1,), (1,)), ((), ())),
                                     preferred_element_type=jnp.float32)
-            part_buf[offset, slot] = value * live
+            part_ref[offset, slot] = value * live
             return carry
 
         lax.fori_loop(begin, begin + size, one_slot, 0)
@@ -100,11 +103,8 @@
                 src_ref=part_buf.at[offset, span], dst_ref=arrived_ref.at[offset, span],
                 send_sem=send_sem.at[offset, chunk], recv_sem=recv_sem.at[offset, chunk],
                 device_id=place(offset), device_id_type=pl.DeviceIdType.MESH)
-        else:
-            copy = pltpu.make_async_copy(
-                part_buf.at[offset, span], arrived_ref.at[offset, span], own_sem.at[chunk])
-        copy.start()
-        copies.append(copy)
+            copy.start()
+            copies.append(copy)
         if chunk == 0:
             if offset != reach:
                 copy = pltpu.make_async_remote_copy(
@@ -113,7 +113,7 @@
                     device_id=place(offset), device_id_type=pl.DeviceIdType.MESH)
             else:
                 copy = pltpu.make_async_copy(
-                    rows_ref.at[reach], arrived_rows_ref.at[reach], own_sem.at[len(spans)])
+                    rows_ref.at[reach], arrived_rows_ref.at[reach], own_sem)
             copy.start()
             copies.append(copy)
     for copy in copies:
@@ -183,8 +183,8 @@
             pltpu.VMEM((num_off, slots, num_flux, block_rows), jnp.float32),
             pltpu.SemaphoreType.DMA((land_blocks,)),
             pltpu.SemaphoreType.DMA((land_blocks,)),
-            pltpu.SemaphoreType.DMA((num_off,)),
-            pltpu.SemaphoreType.DMA((len(spans) + 1,)),
+            pltpu.SemaphoreType.DMA((num_off, len(spans))),
+            pltpu.SemaphoreType.DMA,
             pltpu.SemaphoreType.DMA((num_off, len(spans))),
             pltpu.SemaphoreType.DMA((num_off, len(spans))),
             pltpu.SemaphoreType.DMA((num_off,)),

time: 113 us -> 112 us (level)
  Pallas kernels: 113 us -> 111 us
    pallas_call x1, Pallas kernels: 110 us -> 108 us  [on_device(): pl.pallas_call(functools.partial(exchange_kernel, axes, sizes, spans), ou...]
where the time goes in v4:
time: 112 us; the launch traced here: 111 us
  Pallas kernels  111 us (99%)
    pallas_call x1, Pallas kernels, on_device(): pl.pallas_call(functools.partial(exchange_kernel, axes, sizes, spans), ou...  108 us
    pallas_call x1, Pallas kernels, on_device(): pl.pallas_call(settle_kernel, out_shape=jax.ShapeDtypeStruct((num_kinds,...  2.91 us

profile of v4, /device:TPU:9, one launch (start us, length us, event | category | flops | bytes accessed | tf_op | source)
XLA Modules:
  0.0 111.4 jit_solution(7962684769681654232)
XLA Ops:
  0.0 108.5 %exchange.1 = (f32[7,16,48,256]{3,2,1,0:T(8,128)S(1)}, s32[7,1,16]{2,1,0:T(1,128)S(1)}) custom-call(bf16[4,12,8,4096]{3,2,1,0:T(8,128)(2,1)} %flux_ref.1, f32[8,4096]{1,0:T(8,128)} %frac_ref.1, s32[7,1,16]{2,1,0:T(1,128)} %bitcast.5, s32[1,7]{1,0:T(1,128)} %count_ref.1, s32[7,1,16]{2,1,0:T(1,128)} %bitcast.6, bf16[7,16,256,128]{3,2,1,0:T(8,128)(2,1)} %bitcast.4), custom_call_target="tpu_custom_call" | custom-call | tf_op jit(solution)/shard_map/exchange/pallas_call | solution.py:171
  108.5 2.9 %settle.1 = f32[12,4,12288]{2,1,0:T(4,128)} custom-call(s32[7,1,16]{2,1,0:T(1,128)S(1)} %get-tuple-element.7.rows_ref, f32[7,16,48,256]{3,2,1,0:T(8,128)S(1)} %get-tuple-element.8.arrived_ref), custom_call_target="tpu_custom_call" | custom-call | tf_op jit(solution)/shard_map/settle/pallas_call | solution.py:198

commit v5 on v4

--- a/solution.py
+++ b/solution.py
@@ -10,6 +10,7 @@
 CUTS = 8
 OUT_CUTS = 4
 EARLY = 4
+EDGE = 2
 
 
 def chunk_spans(slots):
@@ -21,12 +22,20 @@
     return spans
 
 
+def flow_orders(reach):
+    far = list(range(reach, 0, -1))
+    both = [sign * away for away in far for sign in (1, -1)]
+    down = [-away for away in far] + far
+    up = far + [-away for away in far]
+    return both, down, up
+
+
 def send_order(reach, spans):
     order = []
-    for away in range(reach, 0, -1):
+    for stage in range(reach):
         for chunk in range(len(spans)):
-            order += [(reach + away, chunk), (reach - away, chunk)]
-    return order + [(reach, chunk) for chunk in range(len(spans))]
+            order += [(2 * stage, chunk), (2 * stage + 1, chunk)]
+    return order + [(2 * reach, chunk) for chunk in range(len(spans))]
 
 
 def exchange_kernel(axes, sizes, spans, flux_ref, frac_ref, col_ref, count_ref, rows_ref,
@@ -41,6 +50,12 @@
     count = sizes[0] * sizes[1]
     me = lax.axis_index(axes[0]) * inner + lax.axis_index(axes[1])
     order = send_order(reach, spans)
+    spot = lax.axis_index(axes[1])
+    offsets = [
+        reach + jnp.where(spot < EDGE, down, jnp.where(spot >= inner - EDGE, up, both))
+        for both, down, up in zip(*flow_orders(reach))
+    ] + [reach]
+    own = num_off - 1
 
     def place(offset):
         there = lax.rem(me + offset - reach + count, count)
@@ -62,11 +77,12 @@
     for load in land_loads:
         load.start()
     loads = {}
-    for offset, chunk in order:
+    for flow, chunk in order:
+        offset = offsets[flow]
         span = pl.ds(*spans[chunk])
-        loads[offset, chunk] = pltpu.make_async_copy(
+        loads[flow, chunk] = pltpu.make_async_copy(
             weights_ref.at[offset, span], weights_buf.at[offset, span],
-            weight_sem.at[offset, chunk])
+            weight_sem.at[flow, chunk])
     for key in order[:EARLY]:
         loads[key].start()
 
@@ -75,10 +91,11 @@
     for key in order[EARLY:]:
         loads[key].start()
     copies = []
-    for offset, chunk in order:
+    for flow, chunk in order:
+        offset = offsets[flow]
         begin, size = spans[chunk]
-        loads[offset, chunk].wait()
-        part_ref = arrived_ref if offset == reach else part_buf
+        loads[flow, chunk].wait()
+        part_ref = arrived_ref if flow == own else part_buf
 
         def one_slot(slot, carry, offset=offset, part_ref=part_ref):
             live = jnp.where(slot < count_ref[0, offset], 1.0, 0.0).astype(jnp.float32)
@@ -98,7 +115,7 @@
         if not copies:
             pl.semaphore_wait(barrier, num_off - 1)
         span = pl.ds(begin, size)
-        if offset != reach:
+        if flow != own:
             copy = pltpu.make_async_remote_copy(
                 src_ref=part_buf.at[offset, span], dst_ref=arrived_ref.at[offset, span],
                 send_sem=send_sem.at[offset, chunk], recv_sem=recv_sem.at[offset, chunk],
@@ -106,7 +123,7 @@
             copy.start()
             copies.append(copy)
         if chunk == 0:
-            if offset != reach:
+            if flow != own:
                 copy = pltpu.make_async_remote_copy(
                     src_ref=rows_ref.at[offset], dst_ref=arrived_rows_ref.at[offset],
                     send_sem=row_send_sem.at[offset], recv_sem=row_recv_sem.at[offset],

time: 112 us -> 112 us (level)
  no operation moved by 1% of the time
where the time goes in v5:
time: 112 us; the launch traced here: 111 us
  Pallas kernels  111 us (99%)
    pallas_call x1, Pallas kernels, on_device(): pl.pallas_call(functools.partial(exchange_kernel, axes, sizes, spans), ou...  109 us
    pallas_call x1, Pallas kernels, on_device(): pl.pallas_call(settle_kernel, out_shape=jax.ShapeDtypeStruct((num_kinds,...  2.91 us

profile of v5, /device:TPU:9, one launch (start us, length us, event | category | flops | bytes accessed | tf_op | source)
XLA Modules:
  0.0 111.4 jit_solution(1989469475315988833)
XLA Ops:
  0.0 108.5 %exchange.1 = (f32[7,16,48,256]{3,2,1,0:T(8,128)S(1)}, s32[7,1,16]{2,1,0:T(1,128)S(1)}) custom-call(bf16[4,12,8,4096]{3,2,1,0:T(8,128)(2,1)} %flux_ref.1, f32[8,4096]{1,0:T(8,128)} %frac_ref.1, s32[7,1,16]{2,1,0:T(1,128)} %bitcast.5, s32[1,7]{1,0:T(1,128)} %count_ref.1, s32[7,1,16]{2,1,0:T(1,128)} %bitcast.6, bf16[7,16,256,128]{3,2,1,0:T(8,128)(2,1)} %bitcast.4), custom_call_target="tpu_custom_call" | custom-call | tf_op jit(solution)/shard_map/exchange/pallas_call | solution.py:188
  108.5 2.9 %settle.1 = f32[12,4,12288]{2,1,0:T(4,128)} custom-call(s32[7,1,16]{2,1,0:T(1,128)S(1)} %get-tuple-element.7.rows_ref, f32[7,16,48,256]{3,2,1,0:T(8,128)S(1)} %get-tuple-element.8.arrived_ref), custom_call_target="tpu_custom_call" | custom-call | tf_op jit(solution)/shard_map/settle/pallas_call | solution.py:215
